TPU v7x, 32 devices: a whole 2x2x4 slice. The times are simulated.
32 devices in a mesh: ctx: 8 (over y, x, core), dp: 4 (over z).
Axes of the slice: x: 2, y: 2, z: 4, core: 2. Of those that a mesh axis runs over, the one named last changes fastest.
Arguments:
- query_previous: bfloat16 [4, 1024, 2048], P('dp', 'ctx'), may hold values from -240 to 240
- key_previous: bfloat16 [4, 1024, 512], P('dp', 'ctx'), may hold values from -6 to 6
- value_previous: bfloat16 [4, 1024, 512], P('dp', 'ctx'), may hold values from -6 to 6
- span_order: int32 [16], replicated, may hold values from 0 to 15, each once
- resid: bfloat16 [4, 1024, 4096], P('dp', 'ctx'), may hold values from -6 to 6
- grad_norm: bfloat16 [4, 1024, 4096], P('dp', 'ctx'), may hold values from -3 to 3
- gain: float32 [4096], replicated, may hold values from 0.1 to 1.9
Outputs:
- out_prev: bfloat16 [4, 1024, 2048], P('dp', 'ctx')
- lse_prev: float32 [4, 16, 1024], P('dp', None, 'ctx')
- resid_grad: bfloat16 [4, 1024, 4096], P('dp', 'ctx')
- gain_grad: float32 [4096], replicated
Inputs may be any that keep to these rules, and one draw needn't show every extreme that they name: span_order names each of the 16 spans once; rows c * 64 to (c + 1) * 64 - 1 of a sequence's arrays hold span span_order[c].
All inputs are finite; a program needn't handle non-finite values.
Results may differ from a plain program's by a relative error of at most 0.0055.
Values may be sent and summed in bfloat16 or wider, within the bound.
No kernel may reach another device: no remote copies, remote signals or barrier semaphores. Data moves between devices by JAX's collectives and lax.ppermute only.
A program may use at most 64 MiB of HBM per device.

v0:
```python
import math
import jax
import jax.numpy as jnp
from jax import lax
from jax.sharding import PartitionSpec as P

QUERY_HEADS = 16
KEY_VALUE_HEADS = 4
HEAD_WIDTH = 128


def key_positions(tally_count, span_order, half):
    index = jnp.arange(tally_count, dtype=jnp.int32)
    slot = index // half
    table = slot[:, None] == jnp.arange(span_order.shape[0], dtype=jnp.int32)[None, :]
    chosen = jnp.sum(jnp.where(table, span_order[None, :], 0), axis=1)
    return chosen * half + index % half


def dense_update(query_rows, q_positions, carry, key_rows, value_rows, k_positions):
    top, total, summed = carry
    scores = jnp.einsum(
        "rkgd,skd->kgrs", query_rows, key_rows, preferred_element_type=jnp.float32
    ) * HEAD_WIDTH ** (-0.5)
    mask = (k_positions[None, :] <= q_positions[:, None])[None, None]
    scores = jnp.where(mask, scores, -1e30)
    new_top = jnp.maximum(top, jnp.max(scores, axis=-1))
    weights = jnp.where(mask, jnp.exp(scores - new_top[..., None]), 0.0)
    factor = jnp.exp(top - new_top)
    total = total * factor + jnp.sum(weights, axis=-1)
    probs = weights.astype(jnp.bfloat16)
    added = jnp.einsum("kgrs,skd->rkgd", probs, value_rows, preferred_element_type=jnp.float32)
    summed = summed * jnp.transpose(factor, (2, 0, 1))[..., None] + added
    return (new_top, total, summed)


def update(query_rows, q_positions, carry, key_rows, value_rows, k_positions):
    later = jnp.min(k_positions) > jnp.max(q_positions)
    return lax.cond(
        later,
        lambda state: state,
        lambda state: dense_update(
            query_rows, q_positions, state, key_rows, value_rows, k_positions
        ),
        carry,
    )


def fold_piece(query_rows, q_positions, carry, k_piece, v_piece, span_order, half):
    tally_count = k_piece.shape[1]
    heads = k_piece.shape[2] // HEAD_WIDTH
    key_rows = k_piece[0].reshape(tally_count, heads, HEAD_WIDTH)
    value_rows = v_piece[0].reshape(tally_count, heads, HEAD_WIDTH)
    k_positions = key_positions(tally_count, span_order, half)
    block = math.gcd(tally_count, 512)
    steps = tally_count // block

    def step_fn(state, items):
        return (update(query_rows, q_positions, state, items[0], items[1], items[2]), None)

    carry, unused = lax.scan(
        step_fn,
        carry,
        (
            key_rows.reshape(steps, block, heads, HEAD_WIDTH),
            value_rows.reshape(steps, block, heads, HEAD_WIDTH),
            k_positions.reshape(steps, block),
        ),
    )
    return carry


def blank_state(heads, query_group, row_indices):
    return (
        jnp.full((heads, query_group, row_indices), -1e30, jnp.float32),
        jnp.zeros((heads, query_group, row_indices), jnp.float32),
        jnp.zeros((row_indices, heads, query_group, HEAD_WIDTH), jnp.float32),
    )


def attention(query_previous, key_previous, value_previous, span_order):
    row_indices = query_previous.shape[1]
    half = row_indices // 2
    query_group = QUERY_HEADS // KEY_VALUE_HEADS
    mine = lax.dynamic_slice_in_dim(span_order, 2 * lax.axis_index("ctx"), 2)
    local = jnp.arange(row_indices, dtype=jnp.int32)
    q_positions = jnp.where(local < half, mine[0], mine[1]) * half + local % half
    query_rows = query_previous[0].reshape(row_indices, KEY_VALUE_HEADS, query_group, HEAD_WIDTH)
    top, total, summed = fold_piece(
        query_rows,
        q_positions,
        blank_state(KEY_VALUE_HEADS, query_group, row_indices),
        lax.all_gather(key_previous, "ctx", axis=1, tiled=True),
        lax.all_gather(value_previous, "ctx", axis=1, tiled=True),
        span_order,
        half,
    )
    output = summed / jnp.transpose(total, (2, 0, 1))[..., None]
    out_prev = output.reshape(1, row_indices, QUERY_HEADS * HEAD_WIDTH).astype(jnp.bfloat16)
    lse_prev = (top + jnp.log(total)).reshape(1, QUERY_HEADS, row_indices)
    return (out_prev, lse_prev)


def norm_backward(resid, grad_norm, gain):
    resid_f = resid[0].astype(jnp.float32)
    grad_f = grad_norm[0].astype(jnp.float32)
    inv_rms = 1.0 / jnp.sqrt(jnp.mean(resid_f * resid_f, axis=-1, keepdims=True) + 1e-05)
    normed = resid_f * inv_rms
    partial_grad = jnp.sum(grad_f * normed, axis=0)
    gain_grad = lax.psum(partial_grad, ("ctx", "dp"))
    scaled = gain[None, :] * grad_f
    resid_grad = (
        (scaled - normed * jnp.mean(scaled * normed, axis=-1, keepdims=True)) * inv_rms
    ).astype(jnp.bfloat16)
    return (gain_grad, resid_grad[None])


def per_device(query_previous, key_previous, value_previous, span_order, resid, grad_norm, gain):
    out_prev, lse_prev = attention(query_previous, key_previous, value_previous, span_order)
    gain_grad, resid_grad = norm_backward(resid, grad_norm, gain)
    return (out_prev, lse_prev, resid_grad, gain_grad)


def solution(mesh):
    return jax.shard_map(
        per_device,
        mesh=mesh,
        in_specs=(
            P("dp", "ctx", None),
            P("dp", "ctx", None),
            P("dp", "ctx", None),
            P(),
            P("dp", "ctx", None),
            P("dp", "ctx", None),
            P(),
        ),
        out_specs=(P("dp", "ctx", None), P("dp", None, "ctx"), P("dp", "ctx", None), P()),
        check_vma=False,
    )
```

profile of v0, /device:TPU:1, one launch (start us, length us, event | category | flops | bytes accessed | tf_op | source)
XLA Modules:
  0.0 89.6 jit_solution(13001923617092184318)
XLA Ops:
  7.2 0.7 all-gather.3.cloned.1.call-update
  8.0 0.7 all-gather.5.cloned.1.call-update
  8.7 0.7 dynamic_slice.27
  9.4 0.6 fusion.49
  10.0 1.3 %copy.20 = bf16[1,128,2048]{1,2,0:T(8,128)(2,1)S(1)} copy(bf16[1,128,2048]{2,1,0:T(8,128)(2,1)} %param.11) | data formatting | bytes 1048576 | tf_op args[0]
  11.3 0.3 copy.22
  11.6 0.7 select_reduce_fusion
  12.4 1.5 %fusion.38 = f32[128]{0:T(128)S(1)} fusion(bf16[1,128,4096]{2,1,0:T(8,128)(2,1)} %param.15), kind=kLoop, calls=%fused_computation.45 | loop fusion | flops 1572736 | bytes 1049088 | tf_op jit(solution)/shard_map/reduce_sum | solution.py:107
  13.9 1.9 %fusion.47 = s32[]{:T(128)} fusion(s32[]{:T(128)} %bitcast.11, s32[]{:T(128)} %bitcast.10), kind=kLoop, calls=%fused_computation.69 | loop fusion | flops 1407 | bytes 12 | tf_op jit(solution)/shard_map/while/body/eval_jaxpr/reduce_max | solution.py:38
  15.9 2.4 %fusion.34 = (f32[4096]{0:T(1024)S(1)}, f32[128]{0:T(128)S(1)}) fusion(bf16[1,128,4096]{2,1,0:T(8,128)(2,1)} %param.15, bf16[1,128,4096]{2,1,0:T(8,128)(2,1)} %param.16, f32[128]{0:T(128)S(1)} %add_rsqrt_fusion, f32[4096]{0:T(1024)} %param.17), kind=kLoop, calls=%fused_computation.41 | loop fusion | flops 4190080 | bytes 2130944 | tf_op jit(solution)/shard_map/reduce_sum | solution.py:109
  18.2 42.3 %psum.7 = f32[4096]{0:T(1024)} all-reduce(f32[4096]{0:T(1024)S(1)} %get-tuple-element.291), channel_id=1, replica_groups=mesh['ctx'=8,'dp'=4] {'ctx','dp'}, use_global_device_ids=true, to_apply=%region_12.13 | all-reduce | flops 4096 | bytes 32768 | tf_op jit(solution)/shard_map/psum | solution.py:110
  60.5 1.5 %fusion.37 = bf16[1,128,4096]{2,1,0:T(8,128)(2,1)} fusion(bf16[1,128,4096]{2,1,0:T(8,128)(2,1)S(1)} %copy-done.1, bf16[1,128,4096]{2,1,0:T(8,128)(2,1)S(1)} %copy-done, f32[128]{0:T(128)S(1)} %broadcast_multiply_fusion.1, f32[128]{0:T(128)S(1)} %add_rsqrt_fusion, f32[4096]{0:T(1024)S(1)} %copy-done.3), kind=kLoop, calls=%fused_computation.44 | loop fusion | flops 4194304 | bytes 3163136 | tf_op jit(solution)/shard_map/convert_element_type | solution.py:114
  62.1 1.3 %reshape_reshape_squeeze.6 = bf16[2,512,4,128]{3,2,1,0:T(4,128)(2,1)S(1)} reshape(bf16[1,1024,512]{2,1,0:T(8,128)(2,1)} %all-gather.3.cloned.1.call-done) | data formatting | bytes 2097152 | tf_op jit(solution)/shard_map/reshape;reshape;squeeze | solution.py:65
  63.6 1.3 %reshape_reshape_squeeze.7 = bf16[2,512,4,128]{3,2,1,0:T(4,128)(2,1)S(1)} reshape(bf16[1,1024,512]{2,1,0:T(8,128)(2,1)} %all-gather.5.cloned.1.call-done) | data formatting | bytes 2097152 | tf_op jit(solution)/shard_map/reshape;reshape;squeeze | solution.py:66
  64.9 1.1 %copy.23 = bf16[2,512,4,128]{3,1,2,0:T(8,128)(2,1)} copy(bf16[2,512,4,128]{3,2,1,0:T(4,128)(2,1)S(1)} %reshape_reshape_squeeze.7) | data formatting | bytes 2097152
  66.2 14.0 %while.16 = (s32[]{:T(128)}, f32[4,4,128]{2,1,0:T(4,128)S(1)}, f32[4,4,128]{2,1,0:T(4,128)S(1)}, f32[128,4,4,128]{3,0,2,1:T(8,128)S(1)}, s32[2,512]{1,0:T(2,128)...) while((s32[]{:T(128)}, f32[4,4,128]{2,1,0:T(4,128)S(1)}, ...), condition=%wide.region_8.9_spmd.clone, body=%wide.region_2.8_spmd.clone.sunk | while | flops 551100160 | bytes 20852624 | solution.py:61
  66.2 0.7 fusion.52
  68.2 5.0 %conditional.3 = ((f32[4,4,128]{2,1,0:T(4,128)S(1)}, f32[4,4,128]{2,1,0:T(4,128)S(1)}, f32[128,4,4,128]{3,0,2,1:T(8,128)S(1)})) conditional(s32[]{:T(128)} %convert_element_type.103, (s32[1,512]{1,0:T(1,128)S(1)}, s32[128]{0:T(128)S(1)}, bf16[2,512,4,128]{3,1,2,0:T(8,128)(2,1)S(1)}, s32[]{:T(128)}, bf16[128,4,4,128]{3,0,2,1:T(8,128)(2,1)S(1)}, ...), branch_computations={%region_4.6_spmd.clone, %region_7.7_spmd} | conditional | flops 551099520 | bytes 20846672 | solution.py:39
  68.2 1.3 %fusion.24 = s32[128]{0:T(128)S(1)} fusion(s32[128]{0:T(128)S(1)} %get-tuple-element.268, s32[128]{0:T(128)S(1)} %get-tuple-element.267, s32[128]{0:T(128)S(1)} %get-tuple-element.272, s32[128]{0:T(128)S(1)} %get-tuple-element.272, s32[128]{0:T(128)S(1)} %get-tuple-element.272, s32[128]{0:T(128)S(1)} %get-tuple-element.272, s32[]{:T(128)} %get-tuple-element.273, ...), kind=kLoop, calls=%fused_computation.25 | loop fusion | flops 1152 | bytes 3596 | tf_op jit(solution)/shard_map/add | solution.py:87
  69.7 0.8 fusion.2
  70.4 1.0 %fusion.4 = f32[4,4,128]{2,1,0:T(4,128)S(1)} fusion(f32[4,512,128,4]{2,1,3,0:T(8,128)S(1)} %get-tuple-element.320, f32[4,4,128]{2,1,0:T(4,128)S(1)} %get-tuple-element.400, pred[128,512]{0,1:T(8,128)(4,1)S(1)} %broadcast_compare_fusion), kind=kLoop, calls=%fused_computation.5 | loop fusion | flops 5240832 | bytes 4276224 | tf_op jit(solution)/shard_map/while/body/eval_jaxpr/cond/branch_0_fun/reduce_sum | solution.py:30
  71.5 1.7 %fusion.11 = f32[128,4,4,128]{3,0,2,1:T(8,128)S(1)} fusion(f32[4,512,128,4]{2,1,3,0:T(8,128)S(1)} %get-tuple-element.320, f32[4,4,128]{2,1,0:T(4,128)S(1)} %get-tuple-element.400, pred[128,512]{0,1:T(8,128)(4,1)S(1)} %broadcast_compare_fusion, f32[128,4,4,128]{3,0,2,1:T(8,128)S(1)} %get-tuple-element.261, bf16[2,512,4,128]{3,1,2,0:T(8,128)(2,1)S(1)} %copy-done.2, ...), kind=kOutput, calls=%fused_computation.9 | convolution fusion | flops 274202624 | bytes 6897668 | tf_op jit(solution)/shard_map/while/body/eval_jaxpr/cond/branch_0_fun/kgrs,skd->rkgd/dot_general | solution.py:32
  73.2 0.7 fusion.52
  75.2 5.0 %conditional.3 = ((f32[4,4,128]{2,1,0:T(4,128)S(1)}, f32[4,4,128]{2,1,0:T(4,128)S(1)}, f32[128,4,4,128]{3,0,2,1:T(8,128)S(1)})) conditional(s32[]{:T(128)} %convert_element_type.103, (s32[1,512]{1,0:T(1,128)S(1)}, s32[128]{0:T(128)S(1)}, bf16[2,512,4,128]{3,1,2,0:T(8,128)(2,1)S(1)}, s32[]{:T(128)}, bf16[128,4,4,128]{3,0,2,1:T(8,128)(2,1)S(1)}, ...), branch_computations={%region_4.6_spmd.clone, %region_7.7_spmd} | conditional | flops 551099520 | bytes 20846672 | solution.py:39
  75.3 1.3 %fusion.24 = s32[128]{0:T(128)S(1)} fusion(s32[128]{0:T(128)S(1)} %get-tuple-element.268, s32[128]{0:T(128)S(1)} %get-tuple-element.267, s32[128]{0:T(128)S(1)} %get-tuple-element.272, s32[128]{0:T(128)S(1)} %get-tuple-element.272, s32[128]{0:T(128)S(1)} %get-tuple-element.272, s32[128]{0:T(128)S(1)} %get-tuple-element.272, s32[]{:T(128)} %get-tuple-element.273, ...), kind=kLoop, calls=%fused_computation.25 | loop fusion | flops 1152 | bytes 3596 | tf_op jit(solution)/shard_map/add | solution.py:87
  76.7 0.8 fusion.2
  77.5 1.0 %fusion.4 = f32[4,4,128]{2,1,0:T(4,128)S(1)} fusion(f32[4,512,128,4]{2,1,3,0:T(8,128)S(1)} %get-tuple-element.320, f32[4,4,128]{2,1,0:T(4,128)S(1)} %get-tuple-element.400, pred[128,512]{0,1:T(8,128)(4,1)S(1)} %broadcast_compare_fusion), kind=kLoop, calls=%fused_computation.5 | loop fusion | flops 5240832 | bytes 4276224 | tf_op jit(solution)/shard_map/while/body/eval_jaxpr/cond/branch_0_fun/reduce_sum | solution.py:30
  78.5 1.7 %fusion.11 = f32[128,4,4,128]{3,0,2,1:T(8,128)S(1)} fusion(f32[4,512,128,4]{2,1,3,0:T(8,128)S(1)} %get-tuple-element.320, f32[4,4,128]{2,1,0:T(4,128)S(1)} %get-tuple-element.400, pred[128,512]{0,1:T(8,128)(4,1)S(1)} %broadcast_compare_fusion, f32[128,4,4,128]{3,0,2,1:T(8,128)S(1)} %get-tuple-element.261, bf16[2,512,4,128]{3,1,2,0:T(8,128)(2,1)S(1)} %copy-done.2, ...), kind=kOutput, calls=%fused_computation.9 | convolution fusion | flops 274202624 | bytes 6897668 | tf_op jit(solution)/shard_map/while/body/eval_jaxpr/cond/branch_0_fun/kgrs,skd->rkgd/dot_general | solution.py:32
  80.2 0.3 divide_convert_fusion
  80.6 0.4 copy.24
  81.0 1.2 %convert_element_type.46 = bf16[1,128,2048]{2,1,0:T(8,128)(2,1)} reshape(bf16[128,4,4,128]{3,2,1,0:T(4,128)(2,1)S(1)} %copy.24) | data formatting | bytes 1048576 | tf_op jit(solution)/shard_map/convert_element_type | solution.py:99
  82.2 0.6 log_add_fusion
  (38 shorter events, 0.7 us)
Async XLA Ops:
  7.2 53.3 %copy-start = (bf16[1,128,4096]{2,1,0:T(8,128)(2,1)S(1)}, bf16[1,128,4096]{2,1,0:T(8,128)(2,1)}, u32[]{:S(2)}) copy-start(bf16[1,128,4096]{2,1,0:T(8,128)(2,1)} %param.15) | copy-start | bytes 3145732
  7.2 53.3 %copy-start.1 = (bf16[1,128,4096]{2,1,0:T(8,128)(2,1)S(1)}, bf16[1,128,4096]{2,1,0:T(8,128)(2,1)}, u32[]{:S(2)}) copy-start(bf16[1,128,4096]{2,1,0:T(8,128)(2,1)} %param.16) | copy-start | bytes 3145732
  7.2 53.3 %copy-start.3 = (f32[4096]{0:T(1024)S(1)}, f32[4096]{0:T(1024)}, u32[]{:S(2)}) copy-start(f32[4096]{0:T(1024)} %param.17) | copy-start | bytes 49156
  7.2 54.9 %all-gather.3.cloned.1.call-start = ((), (), s32[]{:S(2)}) async-start(), calls=%async_computation | async-start | bytes 1179648 | tf_op jit(solution)/shard_map/all_gather | solution.py:93
  7.9 55.6 %all-gather.5.cloned.1.call-start = ((), (), s32[]{:S(2)}) async-start(), calls=%async_computation.1 | async-start | bytes 1179648 | tf_op jit(solution)/shard_map/all_gather | solution.py:94
  69.7 1.8 %copy-start.2 = (bf16[2,512,4,128]{3,1,2,0:T(8,128)(2,1)S(1)}, bf16[2,512,4,128]{3,1,2,0:T(8,128)(2,1)}, u32[]{:S(2)}) copy-start(bf16[2,512,4,128]{3,1,2,0:T(8,128)(2,1)} %get-tuple-element.262) | copy-start | bytes 3145732 | tf_op jit(solution)/shard_map/while/body/eval_jaxpr/cond
  76.7 1.8 %copy-start.2 = (bf16[2,512,4,128]{3,1,2,0:T(8,128)(2,1)S(1)}, bf16[2,512,4,128]{3,1,2,0:T(8,128)(2,1)}, u32[]{:S(2)}) copy-start(bf16[2,512,4,128]{3,1,2,0:T(8,128)(2,1)} %get-tuple-element.262) | copy-start | bytes 3145732 | tf_op jit(solution)/shard_map/while/body/eval_jaxpr/cond
Sparse Core Ops, SparseCore 0:
  9.9 25.9 all-gather.2
  37.7 23.9 all-gather.4
where the time goes:
time: 90.1 us; the launch traced here: 89.6 us
  blocking collectives  42.3 us (47%)
  other arithmetic  15.4 us (17%)
  between operations  14.2 us (16%)
  local copies, waits for them, and re-layouts  8.61 us (10%)
  matrix products  4.87 us (5%)
  loops' own time  2.82 us (3%)
  waiting for transfers between devices  1.4 us (2%)
    psum x1, blocking collectives, norm_backward(): gain_grad = lax.psum(partial_grad, ('ctx', 'dp'))  42.3 us
    dot_general x2, matrix products, dense_update(): jnp.einsum('kgrs,skd->rkgd', probs, value_rows, preferred_element_type=jn...  3.37 us
    unnamed x10, local copies, waits for them, and re-layouts  2.88 us
    another operation x1, loops' own time, fold_piece(): lax.scan(step_fn, carry, (key_rows.reshape(steps, block, heads, HEAD_WIDT...  2.66 us
    add x2, other arithmetic, attention(): jnp.where(local < half, mine[0], mine[1]) * half + local % half  2.54 us
    reduce_sum x1, other arithmetic, norm_backward(): partial_grad = jnp.sum(grad_f * normed, axis=0)  2.36 us
    reduce_sum x2, other arithmetic, dense_update(): total = total * factor + jnp.sum(weights, axis=-1)  2.02 us
    reduce_max x1, other arithmetic, update(): later = jnp.min(k_positions) > jnp.max(q_positions)  1.93 us
  transfers between devices with their start and end apart: 2, of which 0 were waited for; matrix products, arithmetic and copies ran while one was open for 14% of the time, Pallas kernels for 0%

commit v1 on v0

--- a/solution.py
+++ b/solution.py
@@ -7,6 +7,11 @@
 QUERY_HEADS = 16
 KEY_VALUE_HEADS = 4
 HEAD_WIDTH = 128
+
+
+def list_modes(u_in):
+    val = lax.all_gather(u_in, ("ctx", "dp")).sum(axis=0)
+    return val
 
 
 def key_positions(tally_count, span_order, half):
@@ -107,7 +112,7 @@
     inv_rms = 1.0 / jnp.sqrt(jnp.mean(resid_f * resid_f, axis=-1, keepdims=True) + 1e-05)
     normed = resid_f * inv_rms
     partial_grad = jnp.sum(grad_f * normed, axis=0)
-    gain_grad = lax.psum(partial_grad, ("ctx", "dp"))
+    gain_grad = list_modes(partial_grad)
     scaled = gain[None, :] * grad_f
     resid_grad = (
         (scaled - normed * jnp.mean(scaled * normed, axis=-1, keepdims=True)) * inv_rms

time: 90.1 us -> 124 us (1.38)
  the two profiles are of different devices: /device:TPU:1 before, /device:TPU:0 now
where the time goes in v1:
time: 124 us
  blocking collectives  74.1 us (60%)
  other arithmetic  17.1 us (14%)
  between operations  14.2 us (11%)
  local copies, waits for them, and re-layouts  9.5 us (8%)
  matrix products  4.87 us (4%)
  loops' own time  2.82 us (2%)
  waiting for transfers between devices  1.4 us (1%)
    all_gather x1, blocking collectives, list_modes(): val = lax.all_gather(u_in, ('ctx', 'dp')).sum(axis=0)  74.1 us
    dot_general x2, matrix products, dense_update(): jnp.einsum('kgrs,skd->rkgd', probs, value_rows, preferred_element_type=jn...  3.37 us
    unnamed x10, local copies, waits for them, and re-layouts  2.88 us
    another operation x1, loops' own time, fold_piece(): lax.scan(step_fn, carry, (key_rows.reshape(steps, block, heads, HEAD_WIDT...  2.66 us
    add x2, other arithmetic, attention(): jnp.where(local < half, mine[0], mine[1]) * half + local % half  2.54 us
  transfers between devices with their start and end apart: 2, of which 0 were waited for; matrix products, arithmetic and copies ran while one was open for 12% of the time, Pallas kernels for 0%

profile of v1, /device:TPU:0, one launch (start us, length us, event | category | flops | bytes accessed | tf_op | source)
XLA Modules:
  0.0 124.1 jit_solution(17511633943831182959)
XLA Ops:
  7.2 0.7 all-gather.4.cloned.1.call-update
  8.0 0.7 all-gather.6.cloned.1.call-update
  8.7 1.5 %fusion.38 = f32[128]{0:T(128)S(1)} fusion(bf16[1,128,4096]{2,1,0:T(8,128)(2,1)} %param.15), kind=kLoop, calls=%fused_computation.45 | loop fusion | flops 1572736 | bytes 1049088 | tf_op jit(solution)/shard_map/reduce_sum | solution.py:112
  10.2 0.7 select_reduce_fusion
  11.0 2.4 %fusion.34 = (f32[4096]{0:T(1024)S(1)}, f32[128]{0:T(128)S(1)}) fusion(bf16[1,128,4096]{2,1,0:T(8,128)(2,1)} %param.15, bf16[1,128,4096]{2,1,0:T(8,128)(2,1)} %param.16, f32[128]{0:T(128)S(1)} %add_rsqrt_fusion, f32[4096]{0:T(1024)} %param.17), kind=kLoop, calls=%fused_computation.41 | loop fusion | flops 4190080 | bytes 2130944 | tf_op jit(solution)/shard_map/reduce_sum | solution.py:114
  13.3 0.7 dynamic_slice.27
  14.1 1.3 %copy.26 = bf16[1,128,2048]{1,2,0:T(8,128)(2,1)S(1)} copy(bf16[1,128,2048]{2,1,0:T(8,128)(2,1)} %param.11) | data formatting | bytes 1048576 | tf_op args[0]
  15.7 74.1 %all-gather = f32[131072]{0:T(1024)S(1)} all-gather(f32[4096]{0:T(1024)S(1)} %get-tuple-element.302), channel_id=2, replica_groups=mesh['ctx'=8,'dp'=4] {'ctx','dp'}, dimensions={0}, use_global_device_ids=true | all-gather | bytes 540672 | tf_op jit(solution)/shard_map/all_gather | solution.py:13
  89.8 0.9 reshape.127
  90.7 1.7 %reduce_sum.60 = f32[4096]{0:T(1024)} reduce(f32[32,4096]{1,0:T(8,128)} %reshape.127, f32[]{:T(128)} %constant.97.clone.1), dimensions={0}, to_apply=%region_12.13 | reduce | flops 126976 | bytes 540676 | tf_op jit(solution)/shard_map/reduce_sum | solution.py:13
  92.4 0.6 fusion.49
  93.0 1.9 %fusion.47 = s32[]{:T(128)} fusion(s32[]{:T(128)} %bitcast.11, s32[]{:T(128)} %bitcast.10), kind=kLoop, calls=%fused_computation.69 | loop fusion | flops 1407 | bytes 12 | tf_op jit(solution)/shard_map/while/body/eval_jaxpr/reduce_max | solution.py:43
  95.0 1.5 %fusion.37 = bf16[1,128,4096]{2,1,0:T(8,128)(2,1)} fusion(bf16[1,128,4096]{2,1,0:T(8,128)(2,1)S(1)} %copy-done.1, bf16[1,128,4096]{2,1,0:T(8,128)(2,1)S(1)} %copy-done, f32[128]{0:T(128)S(1)} %broadcast_multiply_fusion.1, f32[128]{0:T(128)S(1)} %add_rsqrt_fusion, f32[4096]{0:T(1024)S(1)} %copy-done.3), kind=kLoop, calls=%fused_computation.44 | loop fusion | flops 4194304 | bytes 3163136 | tf_op jit(solution)/shard_map/convert_element_type | solution.py:119
  96.5 1.3 %reshape_reshape_squeeze.6 = bf16[2,512,4,128]{3,2,1,0:T(4,128)(2,1)S(1)} reshape(bf16[1,1024,512]{2,1,0:T(8,128)(2,1)} %all-gather.4.cloned.1.call-done) | data formatting | bytes 2097152 | tf_op jit(solution)/shard_map/reshape;reshape;squeeze | solution.py:70
  98.0 1.3 %reshape_reshape_squeeze.7 = bf16[2,512,4,128]{3,2,1,0:T(4,128)(2,1)S(1)} reshape(bf16[1,1024,512]{2,1,0:T(8,128)(2,1)} %all-gather.6.cloned.1.call-done) | data formatting | bytes 2097152 | tf_op jit(solution)/shard_map/reshape;reshape;squeeze | solution.py:71
  99.4 1.1 copy.29
  100.6 14.0 %while.16 = (s32[]{:T(128)}, f32[4,4,128]{2,1,0:T(4,128)S(1)}, f32[4,4,128]{2,1,0:T(4,128)S(1)}, f32[128,4,4,128]{3,0,2,1:T(8,128)S(1)}, s32[2,512]{1,0:T(2,128)...) while((s32[]{:T(128)}, f32[4,4,128]{2,1,0:T(4,128)S(1)}, ...), condition=%wide.region_8.9_spmd.clone, body=%wide.region_2.8_spmd.clone.sunk | while | flops 551100160 | bytes 20852624 | solution.py:66
  100.7 0.7 fusion.52
  102.7 5.0 %conditional.3 = ((f32[4,4,128]{2,1,0:T(4,128)S(1)}, f32[4,4,128]{2,1,0:T(4,128)S(1)}, f32[128,4,4,128]{3,0,2,1:T(8,128)S(1)})) conditional(s32[]{:T(128)} %convert_element_type.103, (s32[1,512]{1,0:T(1,128)S(1)}, s32[128]{0:T(128)S(1)}, bf16[2,512,4,128]{3,1,2,0:T(8,128)(2,1)S(1)}, s32[]{:T(128)}, bf16[128,4,4,128]{3,0,2,1:T(8,128)(2,1)S(1)}, ...), branch_computations={%region_4.6_spmd.clone, %region_7.7_spmd} | conditional | flops 551099520 | bytes 20846672 | solution.py:44
  102.7 1.3 %fusion.24 = s32[128]{0:T(128)S(1)} fusion(s32[128]{0:T(128)S(1)} %get-tuple-element.279, s32[128]{0:T(128)S(1)} %get-tuple-element.278, s32[128]{0:T(128)S(1)} %get-tuple-element.283, s32[128]{0:T(128)S(1)} %get-tuple-element.283, s32[128]{0:T(128)S(1)} %get-tuple-element.283, s32[128]{0:T(128)S(1)} %get-tuple-element.283, s32[]{:T(128)} %get-tuple-element.284, ...), kind=kLoop, calls=%fused_computation.25 | loop fusion | flops 1152 | bytes 3596 | tf_op jit(solution)/shard_map/add | solution.py:92
  104.1 0.8 fusion.2
  104.9 1.0 fusion.4
  105.9 1.7 %fusion.11 = f32[128,4,4,128]{3,0,2,1:T(8,128)S(1)} fusion(f32[4,512,128,4]{2,1,3,0:T(8,128)S(1)} %get-tuple-element.331, f32[4,4,128]{2,1,0:T(4,128)S(1)} %get-tuple-element.411, pred[128,512]{0,1:T(8,128)(4,1)S(1)} %broadcast_compare_fusion, f32[128,4,4,128]{3,0,2,1:T(8,128)S(1)} %get-tuple-element.272, bf16[2,512,4,128]{3,1,2,0:T(8,128)(2,1)S(1)} %copy-done.2, ...), kind=kOutput, calls=%fused_computation.9 | convolution fusion | flops 274202624 | bytes 6897668 | tf_op jit(solution)/shard_map/while/body/eval_jaxpr/cond/branch_0_fun/kgrs,skd->rkgd/dot_general | solution.py:37
  107.7 0.7 fusion.52
  109.7 5.0 %conditional.3 = ((f32[4,4,128]{2,1,0:T(4,128)S(1)}, f32[4,4,128]{2,1,0:T(4,128)S(1)}, f32[128,4,4,128]{3,0,2,1:T(8,128)S(1)})) conditional(s32[]{:T(128)} %convert_element_type.103, (s32[1,512]{1,0:T(1,128)S(1)}, s32[128]{0:T(128)S(1)}, bf16[2,512,4,128]{3,1,2,0:T(8,128)(2,1)S(1)}, s32[]{:T(128)}, bf16[128,4,4,128]{3,0,2,1:T(8,128)(2,1)S(1)}, ...), branch_computations={%region_4.6_spmd.clone, %region_7.7_spmd} | conditional | flops 551099520 | bytes 20846672 | solution.py:44
  109.7 1.3 %fusion.24 = s32[128]{0:T(128)S(1)} fusion(s32[128]{0:T(128)S(1)} %get-tuple-element.279, s32[128]{0:T(128)S(1)} %get-tuple-element.278, s32[128]{0:T(128)S(1)} %get-tuple-element.283, s32[128]{0:T(128)S(1)} %get-tuple-element.283, s32[128]{0:T(128)S(1)} %get-tuple-element.283, s32[128]{0:T(128)S(1)} %get-tuple-element.283, s32[]{:T(128)} %get-tuple-element.284, ...), kind=kLoop, calls=%fused_computation.25 | loop fusion | flops 1152 | bytes 3596 | tf_op jit(solution)/shard_map/add | solution.py:92
  111.1 0.8 fusion.2
  111.9 1.0 fusion.4
  112.9 1.7 %fusion.11 = f32[128,4,4,128]{3,0,2,1:T(8,128)S(1)} fusion(f32[4,512,128,4]{2,1,3,0:T(8,128)S(1)} %get-tuple-element.331, f32[4,4,128]{2,1,0:T(4,128)S(1)} %get-tuple-element.411, pred[128,512]{0,1:T(8,128)(4,1)S(1)} %broadcast_compare_fusion, f32[128,4,4,128]{3,0,2,1:T(8,128)S(1)} %get-tuple-element.272, bf16[2,512,4,128]{3,1,2,0:T(8,128)(2,1)S(1)} %copy-done.2, ...), kind=kOutput, calls=%fused_computation.9 | convolution fusion | flops 274202624 | bytes 6897668 | tf_op jit(solution)/shard_map/while/body/eval_jaxpr/cond/branch_0_fun/kgrs,skd->rkgd/dot_general | solution.py:37
  115.0 0.4 copy.30
  115.4 1.2 convert_element_type.46
  116.6 0.6 log_add_fusion
  (40 shorter events, 1.4 us)
Async XLA Ops:
  7.2 87.8 %copy-start = (bf16[1,128,4096]{2,1,0:T(8,128)(2,1)S(1)}, bf16[1,128,4096]{2,1,0:T(8,128)(2,1)}, u32[]{:S(2)}) copy-start(bf16[1,128,4096]{2,1,0:T(8,128)(2,1)} %param.15) | copy-start | bytes 3145732
  7.2 87.8 %copy-start.1 = (bf16[1,128,4096]{2,1,0:T(8,128)(2,1)S(1)}, bf16[1,128,4096]{2,1,0:T(8,128)(2,1)}, u32[]{:S(2)}) copy-start(bf16[1,128,4096]{2,1,0:T(8,128)(2,1)} %param.16) | copy-start | bytes 3145732
  7.2 87.8 %copy-start.3 = (f32[4096]{0:T(1024)S(1)}, f32[4096]{0:T(1024)}, u32[]{:S(2)}) copy-start(f32[4096]{0:T(1024)} %param.17) | copy-start | bytes 49156
  7.2 89.3 %all-gather.4.cloned.1.call-start = ((), (), s32[]{:S(2)}) async-start(), calls=%async_computation | async-start | bytes 1179648 | tf_op jit(solution)/shard_map/all_gather | solution.py:98
  7.9 90.1 %all-gather.6.cloned.1.call-start = ((), (), s32[]{:S(2)}) async-start(), calls=%async_computation.1 | async-start | bytes 1179648 | tf_op jit(solution)/shard_map/all_gather | solution.py:99
  104.1 1.8 %copy-start.2 = (bf16[2,512,4,128]{3,1,2,0:T(8,128)(2,1)S(1)}, bf16[2,512,4,128]{3,1,2,0:T(8,128)(2,1)}, u32[]{:S(2)}) copy-start(bf16[2,512,4,128]{3,1,2,0:T(8,128)(2,1)} %get-tuple-element.273) | copy-start | bytes 3145732 | tf_op jit(solution)/shard_map/while/body/eval_jaxpr/cond
  111.1 1.8 %copy-start.2 = (bf16[2,512,4,128]{3,1,2,0:T(8,128)(2,1)S(1)}, bf16[2,512,4,128]{3,1,2,0:T(8,128)(2,1)}, u32[]{:S(2)}) copy-start(bf16[2,512,4,128]{3,1,2,0:T(8,128)(2,1)} %get-tuple-element.273) | copy-start | bytes 3145732 | tf_op jit(solution)/shard_map/while/body/eval_jaxpr/cond
Sparse Core Ops, SparseCore 0:
  9.9 26.2 all-gather.3
  38.1 23.6 all-gather.5
